TPU v7x, 32 devices: a whole 2x2x4 slice. The times are simulated.
32 devices in a mesh: morton: 8 (over z, x), grp: 4 (over y, core).
Axes of the slice: x: 2, y: 2, z: 4, core: 2. Of those that a mesh axis runs over, the one named last changes fastest.
Arguments:
- multipoles: float32 [2048, 152], P(('morton', 'grp')), may hold values from -6 to 6
- chebyshev: float32 [2048, 560], P(('morton', 'grp')), may hold values from -6 to 6
- ghost_rows: int32 [64, 64], P('morton'), may hold values from 0 to 255
- far_src: int32 [2048, 189], P(('morton', 'grp')), may hold values from 0 to 767
- far_kind: int32 [2048, 189], P(('morton', 'grp')), may hold values from 0 to 15
- far_count: int32 [2048], P(('morton', 'grp')), may hold values from 1 to 189
- near_src: int32 [2048, 27], P(('morton', 'grp')), may hold values from 0 to 191, as said below
- near_kind: int32 [2048, 27], P(('morton', 'grp')), may hold values from 0 to 3
- far_ops: float32 [16, 152, 152], replicated, may hold values from -0.046875 to 0.046875
- near_ops: float32 [4, 560, 560], replicated, may hold values from -0.046875 to 0.046875
- local_to_target: float32 [152, 560], replicated, may hold values from -0.5 to 0.5
Outputs:
- potential: float32 [2048, 560], P(('morton', 'grp'))
Inputs may be any that keep to these rules, and one draw needn't show every extreme that they name: Entries below 256 name a box of the target's own range; the others name ghost number far_src - 256 of its far ghost list. Entries below 64 name a box of the target's own device; the others name ghost number near_src - 64 of its range's near ghost list.
All inputs are finite; a program needn't handle non-finite values.
Results may differ from a plain program's by a relative error of at most 0.0003.
Values sent between devices are 32-bit elements; how exact they have to be, the bound alone decides.
No kernel may reach another device: no remote copies, remote signals or barrier semaphores. Data moves between devices by JAX's collectives and lax.ppermute only.
A program may use at most 64 MiB of HBM per device.

v0:
```python
import jax
import jax.numpy as jnp
from jax import lax
from jax.sharding import PartitionSpec as P

NCAP = 16


def class_sum(lookup, indices, weight, class_ids, classes):
    targets, slot_count = indices.shape
    picked = lookup[indices] * weight[:, :, None]
    segment = (jnp.arange(targets, dtype=jnp.int32)[:, None] * classes + class_ids).reshape(-1)
    summed = jax.ops.segment_sum(
        picked.reshape(targets * slot_count, lookup.shape[1]),
        segment,
        num_segments=targets * classes,
    )
    return summed.reshape(targets, classes, lookup.shape[1])


def evaluate(
    far_table,
    near_table,
    far_src,
    far_kind,
    far_count,
    near_src,
    near_kind,
    far_ops,
    near_ops,
    local_to_target,
):
    active = (jnp.arange(far_src.shape[1], dtype=jnp.int32)[None, :] < far_count[:, None]).astype(
        jnp.float32
    )
    far_sum = class_sum(far_table, far_src, active, far_kind, far_ops.shape[0])
    local_field = jnp.einsum("tkp,kpq->tq", far_sum, far_ops, precision=lax.Precision.HIGHEST)
    unit_weight = jnp.ones(near_src.shape, jnp.float32)
    near_sum = class_sum(near_table, near_src, unit_weight, near_kind, near_ops.shape[0])
    near_field = jnp.einsum("tkc,kcd->td", near_sum, near_ops, precision=lax.Precision.HIGHEST)
    return jnp.dot(local_field, local_to_target, precision=lax.Precision.HIGHEST) + near_field


def shards(
    multipoles,
    chebyshev,
    ghost_rows,
    far_src,
    far_kind,
    far_count,
    near_src,
    near_kind,
    far_ops,
    near_ops,
    local_to_target,
):
    width_p = multipoles.shape[1]
    width_q = chebyshev.shape[1]
    range_multi, range_cheb = (
        lax.all_gather(multipoles, "grp", axis=0, tiled=True),
        lax.all_gather(chebyshev, "grp", axis=0, tiled=True),
    )
    near_slots = NCAP
    near_rows = ghost_rows[:, :near_slots]
    ghost_multi, ghost_cheb = (
        lax.all_to_all(range_multi[ghost_rows], "morton", split_axis=0, concat_axis=0, tiled=True),
        lax.all_to_all(range_cheb[near_rows], "morton", split_axis=0, concat_axis=0, tiled=True),
    )
    far_table = jnp.concatenate([range_multi, ghost_multi.reshape(-1, width_p)], axis=0)
    near_table = jnp.concatenate([chebyshev, ghost_cheb.reshape(-1, width_q)], axis=0)
    targets = far_src.shape[0]
    block_rows = min(128, targets)
    num_blocks = targets // block_rows
    pieces = (
        far_src.reshape(num_blocks, block_rows, -1),
        far_kind.reshape(num_blocks, block_rows, -1),
        far_count.reshape(num_blocks, block_rows),
        near_src.reshape(num_blocks, block_rows, -1),
        near_kind.reshape(num_blocks, block_rows, -1),
    )

    def run_block(parts):
        return evaluate(
            far_table,
            near_table,
            parts[0],
            parts[1],
            parts[2],
            parts[3],
            parts[4],
            far_ops,
            near_ops,
            local_to_target,
        )

    result = lax.map(run_block, pieces)
    return result.reshape(targets, width_q)


def solution(mesh):
    in_specs = (
        P(("morton", "grp"), None),
        P(("morton", "grp"), None),
        P("morton", None),
        P(("morton", "grp"), None),
        P(("morton", "grp"), None),
        P(("morton", "grp")),
        P(("morton", "grp"), None),
        P(("morton", "grp"), None),
        P(),
        P(),
        P(),
    )
    out_specs = P(("morton", "grp"), None)
    return jax.shard_map(shards, mesh=mesh, in_specs=in_specs, out_specs=out_specs, check_vma=False)
```

profile of v0, /device:TPU:0, one launch (start us, length us, event | category | flops | bytes accessed | tf_op | source)
XLA Modules:
  0.0 232.5 jit_solution(3093291289267172083)
XLA Ops:
  0.0 0.0 copy-start
  0.0 0.0 copy-start.1
  0.0 9.7 %all_gather.7 = f32[256,560]{1,0:T(8,128)S(1)} all-gather(f32[64,560]{1,0:T(8,128)} %param.12), channel_id=1, replica_groups=mesh['morton'=8,'grp'=4] {'grp'}, dimensions={0}, use_global_device_ids=true | all-gather | bytes 716800 | tf_op jit(solution)/shard_map/all_gather | solution.py:61
  9.7 0.7 compare_select_fusion.2
  10.4 0.1 reshape.141
  10.5 1.5 gather_fusion.1
  12.0 5.8 %all-to-all-start.1 = ((f32[8,16,560]{2,1,0:T(8,128)}), f32[8,16,560]{2,1,0:T(8,128)S(1)}, u32[]{:S(2)}, u32[]{:S(2)}) async-start(f32[8,16,560]{2,1,0:T(8,128)} %bitcast.4), calls=%async_computation.1 | async-start | bytes 655360 | tf_op jit(solution)/shard_map/all_to_all | solution.py:67
  17.8 0.9 compare_select_fusion
  18.7 0.7 fusion.9
  19.4 0.7 compare_select_fusion.1
  20.1 0.9 broadcast_add_fusion
  21.1 0.7 broadcast_add_fusion.1
  21.8 0.7 compare_select_fusion.3
  22.5 0.1 reshape.125
  22.6 0.2 reshape.133
  22.8 0.8 reshape.157
  23.6 0.8 reshape.122
  24.4 0.1 copy.13
  24.5 0.1 reshape.149
  24.6 0.1 copy.12
  24.7 0.1 reshape.165
  24.8 6.0 %all_gather.6 = f32[256,152]{1,0:T(8,128)S(1)} all-gather(f32[64,152]{1,0:T(8,128)} %param.11), channel_id=1, replica_groups=mesh['morton'=8,'grp'=4] {'grp'}, dimensions={0}, use_global_device_ids=true | all-gather | bytes 194560 | tf_op jit(solution)/shard_map/all_gather | solution.py:60
  30.8 2.2 gather_fusion
  33.1 0.6 pad_clamp_fusion
  33.7 0.0 all-to-all-done.1
  33.7 6.0 %all-to-all-start = ((f32[8,64,152]{2,1,0:T(8,128)}), f32[8,64,152]{2,1,0:T(8,128)}, u32[]{:S(2)}, u32[]{:S(2)}) async-start(f32[8,64,152]{2,1,0:T(8,128)} %bitcast), calls=%async_computation | async-start | bytes 1048576 | tf_op jit(solution)/shard_map/all_to_all | solution.py:66
  39.7 0.0 copy-done.1
  39.7 0.8 pad_maximum_fusion.1
  40.5 30.5 %scatter_custom_fusion.1 = f32[256,560]{1,0:T(8,128)} fusion(s32[1728]{0:T(1024)S(1)} %reshape.165, f32[192,560]{1,0:T(8,128)} %pad_maximum_fusion.1, s32[2048]{0:T(1024)S(1)} %pad_clamp_fusion.1, f32[]{:T(128)} %constant.13.clone.1), kind=kCustom, calls=%fused_computation.9 | custom fusion | flops 967680 | bytes 573952 | tf_op jit(solution)/shard_map/while/body/eval_jaxpr/scatter-add | solution.py:13
  71.0 1.3 reshape.121
  72.3 6.7 %convolution_bitcast_fusion = f32[64,560]{1,0:T(8,128)} fusion(f32[4,560,560]{2,1,0:T(8,128)} %param.20, f32[64,4,560]{2,1,0:T(4,128)S(1)} %reshape.121), kind=kOutput, calls=%fused_computation.11 | convolution fusion | flops 963379200 | bytes 5734400 | tf_op jit(solution)/shard_map/while/body/eval_jaxpr/tkc,kcd->td/dot_general | solution.py:40
  79.0 0.0 all-to-all-done
  79.0 2.0 pad_maximum_fusion
  81.0 147.1 %scatter_custom_fusion = f32[1024,152]{1,0:T(8,128)S(1)} fusion(s32[12096]{0:T(1024)} %reshape.157, f32[12096]{0:T(1024)} %reshape.122, f32[]{:T(128)} %constant.13.clone.1, f32[768,152]{1,0:T(8,128)} %pad_maximum_fusion, s32[12288]{0:T(1024)} %pad_clamp_fusion), kind=kCustom, calls=%fused_computation.6 | custom fusion | flops 3677184 | bytes 1507840 | tf_op jit(solution)/shard_map/while/body/eval_jaxpr/scatter-add | solution.py:13
  228.1 0.0 copy-done
  228.1 2.3 %convolution_bitcast_fusion.1 = f32[64,152]{1,0:T(8,128)S(1)} fusion(f32[16,152,152]{2,1,0:T(8,128)S(1)} %copy-done, f32[64,16,152]{2,1,0:T(8,128)S(1)} %bitcast.13), kind=kOutput, calls=%fused_computation.13 | convolution fusion | flops 283901952 | bytes 2140160 | tf_op jit(solution)/shard_map/while/body/eval_jaxpr/tkp,kpq->tq/dot_general | solution.py:37
  230.4 2.1 convolution_add_fusion
  (5 shorter events, 0.0 us)
Async XLA Ops:
  0.0 228.1 %copy-start = (f32[16,152,152]{2,1,0:T(8,128)S(1)}, f32[16,152,152]{2,1,0:T(8,128)}, u32[]{:S(2)}) copy-start(f32[16,152,152]{2,1,0:T(8,128)} %param.19) | copy-start | bytes 4435972
  0.0 39.7 %copy-start.1 = (f32[64,560]{1,0:T(8,128)S(1)}, f32[64,560]{1,0:T(8,128)}, u32[]{:S(2)}) copy-start(f32[64,560]{1,0:T(8,128)} %param.12) | copy-start | bytes 430084
  12.0 21.7 %all-to-all-start.1 = ((f32[8,16,560]{2,1,0:T(8,128)}), f32[8,16,560]{2,1,0:T(8,128)S(1)}, u32[]{:S(2)}, u32[]{:S(2)}) async-start(f32[8,16,560]{2,1,0:T(8,128)} %bitcast.4), calls=%async_computation.1 | async-start | bytes 655360 | tf_op jit(solution)/shard_map/all_to_all | solution.py:67
  33.7 45.3 %all-to-all-start = ((f32[8,64,152]{2,1,0:T(8,128)}), f32[8,64,152]{2,1,0:T(8,128)}, u32[]{:S(2)}, u32[]{:S(2)}) async-start(f32[8,64,152]{2,1,0:T(8,128)} %bitcast), calls=%async_computation | async-start | bytes 1048576 | tf_op jit(solution)/shard_map/all_to_all | solution.py:66
where the time goes:
time: 234 us; the launch traced here: 232 us
  other arithmetic  186 us (79%)
  blocking collectives  15.7 us (7%)
  starting transfers between devices  11.8 us (5%)
  matrix products  11.1 us (5%)
  local copies, waits for them, and re-layouts  7.46 us (3%)
    scatter-add x2, other arithmetic, class_sum(): jax.ops.segment_sum(picked.reshape(targets * slot_count, lookup.shape[1])...  178 us
    all_gather x1, blocking collectives, shards(): lax.all_gather(chebyshev, 'grp', axis=0, tiled=True)  9.72 us
    dot_general x1, matrix products, evaluate(): jnp.einsum('tkc,kcd->td', near_sum, near_ops, precision=lax.Precision.HIG...  6.7 us
    all_gather x1, blocking collectives, shards(): lax.all_gather(multipoles, 'grp', axis=0, tiled=True)  5.99 us
    all_to_all x1, starting transfers between devices, shards(): lax.all_to_all(range_multi[ghost_rows], 'morton', split_axis=0, concat_ax...  5.99 us
    all_to_all x1, starting transfers between devices, shards(): lax.all_to_all(range_cheb[near_rows], 'morton', split_axis=0, concat_axis...  5.81 us
  transfers between devices with their start and end apart: 2, of which 0 were waited for; matrix products, arithmetic and copies ran while one was open for 21% of the time, Pallas kernels for 0%

commit v1 on v0

v1 whole, which is shorter than its diff:
```python
import functools

import jax
import jax.numpy as jnp
from jax import lax
from jax.experimental import pallas as pl
from jax.experimental.pallas import tpu as pltpu
from jax.sharding import PartitionSpec as P

NCAP = 16
LANES = 128
F32 = jnp.float32
BF16 = jnp.bfloat16


def cdiv(a, b):
    return -(-a // b)


def split(x):
    hi = x.astype(BF16)
    return hi, (x - hi.astype(F32)).astype(BF16)


def mm(a, b):
    return lax.dot_general(a, b, (((1,), (0,)), ((), ())), preferred_element_type=F32)


def counts_kernel(dims, cnt_ref, fsrc_ref, fkind_ref, nsrc_ref, nkind_ref, fops_ref, nops_ref, l2t_ref,
                  wf_ref, wn_ref, fh_ref, fl_ref, nh_ref, nl_ref, lh_ref, ll_ref, c_ref, lo_ref):
    targets, far, near, fcls, ncls, fhi, nhi, rows, slots, near_at, nrows = dims
    group = 4
    fsrc = fsrc_ref[...]
    nsrc = nsrc_ref[...]
    c_ref[...] = jnp.full(c_ref.shape, -1, jnp.int32)
    lo_ref[...] = jnp.zeros(lo_ref.shape, jnp.int32)
    c_ref[:, :far] = (fsrc >> 7) * fcls + fkind_ref[...]
    lo_ref[:, :far] = fsrc & (LANES - 1)
    c_ref[:, near_at:near_at + near] = fhi * fcls + (nsrc >> 7) * ncls + nkind_ref[...]
    lo_ref[:, near_at:near_at + near] = nsrc & (LANES - 1)
    lane = lax.broadcasted_iota(jnp.int32, (1, slots), 1)
    row_id = lax.broadcasted_iota(jnp.int32, (rows, slots), 0)
    lo_id = lax.broadcasted_iota(jnp.int32, (LANES, slots), 0)

    def body(step, carry):
        for i in range(group):
            t = step * group + i
            live = (lane < cnt_ref[t]) | (lane >= near_at)
            c_row = jnp.where(live, c_ref[pl.ds(t, 1), :], -1)
            one_c = jnp.where(row_id == c_row, 1.0, 0.0).astype(BF16)
            one_lo = jnp.where(lo_id == lo_ref[pl.ds(t, 1), :], 1.0, 0.0).astype(BF16)
            w = lax.dot_general(one_c, one_lo, (((1,), (1,)), ((), ())), preferred_element_type=F32)
            at = pl.multiple_of(t * fcls, fcls)
            for h in range(fhi):
                wf_ref[pl.ds(at, fcls), h * LANES:(h + 1) * LANES] = w[h * fcls:(h + 1) * fcls].astype(BF16)
            wn_ref[pl.ds(pl.multiple_of(t * nrows, nrows), nrows), :] = w[fhi * fcls:fhi * fcls + nrows]
        return carry

    lax.fori_loop(0, targets // group, body, 0)
    for k in range(fcls):
        fh_ref[k], fl_ref[k] = split(fops_ref[k])
    for k in range(ncls):
        nh_ref[k], nl_ref[k] = split(nops_ref[k])
    lh_ref[...], ll_ref[...] = split(l2t_ref[...])


def dot3(x, wh, wl):
    xh, xl = split(x)
    both = mm(jnp.concatenate([xh, xl], axis=0), wh)
    n = x.shape[0]
    return both[:n] + both[n:] + mm(xh, wl)


def field_kernel(dims, wf_ref, wn_ref, fh_ref, fl_ref, nh_ref, nl_ref, lh_ref, ll_ref,
                 rm_ref, gm_ref, oc_ref, gc_ref, out_ref, fs_ref):
    targets, far, near, fcls, ncls, fhi, nhi, rows, slots, near_at, nrows = dims
    own = rm_ref.shape[0]
    ghosts = gm_ref.shape[0]
    rh, rl = split(rm_ref[...])
    gh, gl = split(gm_ref[...])
    wr = wf_ref[:, :own]
    wg = wf_ref[:, own:own + ghosts]
    width = rm_ref.shape[1]
    far_sum = mm(wr, rh) + mm(wr, rl) + mm(wg, gh) + mm(wg, gl)
    cuts = [(at, min(at + LANES, width)) for at in range(0, width, LANES)]
    for i, (first, last) in enumerate(cuts):
        fs_ref[i, :, :last - first] = far_sum[:, first:last]
    local = jnp.zeros((targets, width), F32)
    for k in range(fcls):
        x = jnp.concatenate(
            [fs_ref[i, pl.ds(k, targets, stride=fcls), :][:, :last - first] for i, (first, last) in enumerate(cuts)],
            axis=1)
        local += dot3(x, fh_ref[k], fl_ref[k])
    acc = dot3(local, lh_ref[...], ll_ref[...])
    table = jnp.concatenate([oc_ref[...], gc_ref[...]], axis=0)
    th, tl = split(table)
    length = table.shape[0]
    sums = jnp.zeros((ncls * targets, table.shape[1]), F32)
    for h in range(nhi):
        first, last = h * LANES, min((h + 1) * LANES, length)
        w = jnp.concatenate(
            [wn_ref[pl.ds(h * ncls + k, targets, stride=nrows), :] for k in range(ncls)], axis=0
        ).astype(BF16)[:, :last - first]
        sums += mm(w, th[first:last]) + mm(w, tl[first:last])
    for k in range(ncls):
        acc += dot3(sums[k * targets:(k + 1) * targets], nh_ref[k], nl_ref[k])
    out_ref[...] = acc


def shards(multipoles, chebyshev, ghost_rows, far_src, far_kind, far_count, near_src, near_kind,
           far_ops, near_ops, local_to_target):
    targets, width_p = multipoles.shape
    width_q = chebyshev.shape[1]
    fcls, ncls = far_ops.shape[0], near_ops.shape[0]
    far, near = far_src.shape[1], near_src.shape[1]
    range_multi = lax.all_gather(multipoles, "grp", axis=0, tiled=True)
    range_cheb = lax.all_gather(chebyshev, "grp", axis=0, tiled=True)
    near_rows = ghost_rows[:, :NCAP]
    ghost_multi = lax.all_to_all(range_multi[ghost_rows], "morton", split_axis=0, concat_axis=0, tiled=True)
    ghost_cheb = lax.all_to_all(range_cheb[near_rows], "morton", split_axis=0, concat_axis=0, tiled=True)
    ghost_multi = ghost_multi.reshape(-1, width_p)
    ghost_cheb = ghost_cheb.reshape(-1, width_q)

    ftable = range_multi.shape[0] + ghost_multi.shape[0]
    ntable = targets + ghost_cheb.shape[0]
    fhi, nhi = cdiv(ftable, LANES), cdiv(ntable, LANES)
    nrows = cdiv(nhi * ncls, 8) * 8
    rows = cdiv(fhi * fcls + nrows, 16) * 16
    near_at = cdiv(far, 64) * 64
    slots = cdiv(near_at + near, LANES) * LANES
    dims = (targets, far, near, fcls, ncls, fhi, nhi, rows, slots, near_at, nrows)

    def like(x):
        return jax.ShapeDtypeStruct(x.shape, BF16)

    vmem = pl.BlockSpec(memory_space=pltpu.VMEM)
    smem = pl.BlockSpec(memory_space=pltpu.SMEM)
    parts = pl.pallas_call(
        functools.partial(counts_kernel, dims),
        out_shape=(
            jax.ShapeDtypeStruct((targets * fcls, fhi * LANES), BF16),
            jax.ShapeDtypeStruct((targets * nrows, LANES), F32),
            like(far_ops), like(far_ops), like(near_ops), like(near_ops),
            like(local_to_target), like(local_to_target),
        ),
        in_specs=[smem] + [vmem] * 7,
        out_specs=(vmem,) * 8,
        scratch_shapes=[pltpu.VMEM((targets, slots), jnp.int32), pltpu.VMEM((targets, slots), jnp.int32)],
        name="counts",
    )(far_count, far_src, far_kind, near_src, near_kind, far_ops, near_ops, local_to_target)
    return pl.pallas_call(
        functools.partial(field_kernel, dims),
        out_shape=jax.ShapeDtypeStruct((targets, width_q), F32),
        in_specs=[vmem] * 12,
        out_specs=vmem,
        scratch_shapes=[pltpu.VMEM((cdiv(width_p, LANES), targets * fcls, LANES), F32)],
        name="field",
    )(*parts, range_multi, ghost_multi, chebyshev, ghost_cheb)


def solution(mesh):
    both = P(("morton", "grp"), None)
    in_specs = (both, both, P("morton", None), both, both, P(("morton", "grp")), both, both, P(), P(), P())
    return jax.shard_map(shards, mesh=mesh, in_specs=in_specs, out_specs=both, check_vma=False)
```

time: 234 us -> 57.8 us (0.25)
  other arithmetic: 186 us -> 0.78 us
  Pallas kernels: 0 us -> 21.3 us
  matrix products: 11.1 us -> 0 us
  waiting for transfers between devices: 0.01 us -> 4.42 us
  starting transfers between devices: 11.8 us -> 9.44 us
    scatter-add x2 -> x0, other arithmetic: 178 us -> none  [class_sum(): jax.ops.segment_sum(picked.reshape(targets * slot_count, lookup.shape[1])...]
    pallas_call x0 -> x2, Pallas kernels: none -> 21.3 us  [the longest x1 11.5 us: shards(): pl.pallas_call(functools.partial(counts_kernel, dims), out_shape=(jax.Sha...]
    dot_general x3 -> x0, matrix products: 11.1 us -> none  [the longest x1 6.7 us: evaluate(): jnp.einsum('tkc,kcd->td', near_sum, near_ops, precision=lax.Precision.HIG...]
    concatenate x2 -> x0, other arithmetic: 2.81 us -> none  [the longest x1 1.98 us: shards(): jnp.concatenate([range_multi, ghost_multi.reshape(-1, width_p)], axis=0)]
    all_to_all x1, waiting for transfers between devices: 0.01 us -> 2.66 us  [shards(): lax.all_to_all(range_cheb[near_rows], 'morton', split_axis=0, concat_axis...]
    all_to_all x1, starting transfers between devices: 5.99 us -> 3.64 us  [shards(): lax.all_to_all(range_multi[ghost_rows], 'morton', split_axis=0, concat_ax...]
  transfers between devices with their start and end apart: 2 -> 2, of which waited for: 0 -> 2; matrix products, arithmetic and copies ran while one was open for 21% -> 6% of each run, Pallas kernels for 0% -> 20%
where the time goes in v1:
time: 57.8 us; the launch traced here: 57.5 us
  Pallas kernels  21.3 us (37%)
  blocking collectives  15.4 us (27%)
  starting transfers between devices  9.44 us (16%)
  local copies, waits for them, and re-layouts  6.12 us (11%)
  waiting for transfers between devices  4.42 us (8%)
  other arithmetic  0.78 us (1%)
    pallas_call x1, Pallas kernels, shards(): pl.pallas_call(functools.partial(counts_kernel, dims), out_shape=(jax.Sha...  11.5 us
    pallas_call x1, Pallas kernels, shards(): pl.pallas_call(functools.partial(field_kernel, dims), out_shape=jax.Shape...  9.78 us
    all_gather x1, blocking collectives, shards(): range_cheb = lax.all_gather(chebyshev, 'grp', axis=0, tiled=True)  9.6 us
    all_to_all x1, starting transfers between devices, shards(): lax.all_to_all(range_cheb[near_rows], 'morton', split_axis=0, concat_axis...  5.81 us
    all_gather x1, blocking collectives, shards(): range_multi = lax.all_gather(multipoles, 'grp', axis=0, tiled=True)  5.76 us
    all_to_all x1, starting transfers between devices, shards(): lax.all_to_all(range_multi[ghost_rows], 'morton', split_axis=0, concat_ax...  3.64 us
    all_to_all x1, waiting for transfers between devices, shards(): lax.all_to_all(range_cheb[near_rows], 'morton', split_axis=0, concat_axis...  2.66 us
    gather x1, local copies, waits for them, and re-layouts, shards(): range_multi[ghost_rows]  2.24 us
  transfers between devices with their start and end apart: 2, of which 2 were waited for; matrix products, arithmetic and copies ran while one was open for 6% of the time, Pallas kernels for 20%

profile of v1, /device:TPU:0, one launch (start us, length us, event | category | flops | bytes accessed | tf_op | source)
XLA Modules:
  0.0 57.5 jit_solution(18117839846955248002)
XLA Ops:
  0.0 0.0 copy-start.6
  0.0 0.0 copy-start.3
  0.0 0.8 %compare_select_fusion = s32[8,16]{1,0:T(8,128)S(1)} fusion(s32[8,64]{1,0:T(8,128)} %param.13), kind=kLoop, calls=%fused_computation.2 | loop fusion | flops 384 | bytes 1024 | tf_op jit(solution)/shard_map/select_n | solution.py:120
  0.8 0.1 reshape.18
  0.9 9.6 %all_gather.7 = f32[256,560]{1,0:T(8,128)S(1)} all-gather(f32[64,560]{1,0:T(8,128)} %oc_ref.1), channel_id=1, replica_groups=mesh['morton'=8,'grp'=4] {'grp'}, dimensions={0}, use_global_device_ids=true | all-gather | bytes 716800 | tf_op jit(solution)/shard_map/all_gather | solution.py:117
  10.5 1.5 %gather_fusion.1 = f32[128,560]{1,0:T(8,128)} fusion(f32[256,560]{1,0:T(8,128)S(1)} %all_gather.7, s32[1024]{0:T(1024)S(1)} %pad_clamp_fusion), kind=kCustom, calls=%fused_computation.1 | custom fusion | bytes 573952 | tf_op jit(solution)/shard_map/gather | solution.py:120
  12.0 5.8 %all-to-all-start.1 = ((f32[8,16,560]{2,1,0:T(8,128)}), f32[8,16,560]{2,1,0:T(8,128)S(1)}, u32[]{:S(2)}, u32[]{:S(2)}) async-start(f32[8,16,560]{2,1,0:T(8,128)} %bitcast.2), calls=%async_computation.1 | async-start | bytes 655360 | tf_op jit(solution)/shard_map/all_to_all | solution.py:120
  17.8 0.0 copy-done.6
  17.8 0.1 reshape.10
  17.9 0.0 copy-done.3
  17.9 5.8 %all_gather.6.rm_ref = f32[256,152]{1,0:T(8,128)S(1)} all-gather(f32[64,152]{1,0:T(8,128)S(1)} %copy-done.3), channel_id=1, replica_groups=mesh['morton'=8,'grp'=4] {'grp'}, dimensions={0}, use_global_device_ids=true | all-gather | bytes 194560 | tf_op jit(solution)/shard_map/all_gather | solution.py:116
  23.7 0.0 copy-start
  23.7 0.0 copy-start.4
  23.7 0.0 copy-start.5
  23.7 2.2 %gather_fusion = f32[512,152]{1,0:T(8,128)} fusion(f32[256,152]{1,0:T(8,128)S(1)} %all_gather.6.rm_ref, s32[1024]{0:T(1024)S(1)} %pad_clamp_fusion.1), kind=kCustom, calls=%fused_computation | custom fusion | bytes 624640 | tf_op jit(solution)/shard_map/gather | solution.py:119
  25.9 2.7 %all-to-all-done.1 = f32[8,16,560]{2,1,0:T(8,128)S(1)} async-done(((f32[8,16,560]{2,1,0:T(8,128)}), f32[8,16,560]{2,1,0:T(8,128)S(1)}, u32[]{:S(2)}, u32[]{:S(2)}) %all-to-all-start.1) | async-done | bytes 286752 | tf_op jit(solution)/shard_map/all_to_all | solution.py:120
  28.6 0.0 copy-start.2
  28.6 0.0 copy-done
  28.6 3.6 %all-to-all-start = ((f32[8,64,152]{2,1,0:T(8,128)}), f32[8,64,152]{2,1,0:T(8,128)S(1)}, u32[]{:S(2)}, u32[]{:S(2)}) async-start(f32[8,64,152]{2,1,0:T(8,128)} %bitcast), calls=%async_computation | async-start | bytes 1048576 | tf_op jit(solution)/shard_map/all_to_all | solution.py:119
  32.2 0.0 copy-done.4
  32.2 0.7 %copy.12.nsrc_ref = s32[64,27]{1,0:T(8,128)} copy(s32[64,27]{0,1:T(8,128)S(1)} %copy-done.4) | data formatting | bytes 13824 | tf_op args[6]
  32.9 0.0 copy-done.5
  32.9 0.7 %copy.13.nkind_ref = s32[64,27]{1,0:T(8,128)} copy(s32[64,27]{0,1:T(8,128)S(1)} %copy-done.5) | data formatting | bytes 13824 | tf_op args[7]
  33.6 11.5 %counts.1 = (bf16[1024,768]{1,0:T(8,128)(2,1)}, f32[512,128]{1,0:T(8,128)}, bf16[16,152,152]{2,1,0:T(8,128)(2,1)}, bf16[16,152,152]{2,1,0:T(8,128)(2,1)}, bf16[4...) custom-call(s32[64]{0:T(128)} %cnt_ref.1, ...), custom_call_target="tpu_custom_call" | custom-call | tf_op jit(solution)/shard_map/counts/pallas_call | solution.py:138
  45.2 0.0 copy-done.2
  45.2 1.8 %all-to-all-done = f32[8,64,152]{2,1,0:T(8,128)S(1)} async-done(((f32[8,64,152]{2,1,0:T(8,128)}), f32[8,64,152]{2,1,0:T(8,128)S(1)}, u32[]{:S(2)}, u32[]{:S(2)}) %all-to-all-start) | async-done | bytes 311328 | tf_op jit(solution)/shard_map/all_to_all | solution.py:119
  46.9 0.0 copy-start.1
  46.9 0.8 %copy-done.1 = f32[8,64,152]{2,1,0:T(8,128)} copy-done((f32[8,64,152]{2,1,0:T(8,128)}, f32[8,64,152]{2,1,0:T(8,128)S(1)}, u32[]{:S(2)}) %copy-start.1) | copy-done | bytes 311320
  47.7 9.8 %field.1 = f32[64,560]{1,0:T(8,128)} custom-call(bf16[1024,768]{1,0:T(8,128)(2,1)} %get-tuple-element.13.wf_ref, f32[512,128]{1,0:T(8,128)} %get-tuple-element.14.wn_ref, bf16[16,152,152]{2,1,0:T(8,128)(2,1)} %get-tuple-element.15.fh_ref, bf16[16,152,152]{2,1,0:T(8,128)(2,1)} %get-tuple-element.16.fl_ref, bf16[4,560,560]{2,1,0:T(8,128)(2,1)} %get-tuple-element.17.nh_ref, ...), custom_call_target="tpu_custom_call" | custom-call | tf_op jit(solution)/shard_map/field/pallas_call | solution.py:151
  (3 shorter events, 0.0 us)
Async XLA Ops:
  0.0 17.8 %copy-start.6 = (s32[8,64]{1,0:T(8,128)S(1)}, s32[8,64]{1,0:T(8,128)}, u32[]{:S(2)}) copy-start(s32[8,64]{1,0:T(8,128)} %param.13) | copy-start | bytes 6148
  0.0 17.9 %copy-start.3 = (f32[64,152]{1,0:T(8,128)S(1)}, f32[64,152]{1,0:T(8,128)}, u32[]{:S(2)}) copy-start(f32[64,152]{1,0:T(8,128)} %param.11) | copy-start | bytes 116740
  12.0 16.6 %all-to-all-start.1 = ((f32[8,16,560]{2,1,0:T(8,128)}), f32[8,16,560]{2,1,0:T(8,128)S(1)}, u32[]{:S(2)}, u32[]{:S(2)}) async-start(f32[8,16,560]{2,1,0:T(8,128)} %bitcast.2), calls=%async_computation.1 | async-start | bytes 655360 | tf_op jit(solution)/shard_map/all_to_all | solution.py:120
  23.7 4.9 %copy-start = (f32[256,152]{1,0:T(8,128)}, f32[256,152]{1,0:T(8,128)S(1)}, u32[]{:S(2)}) copy-start(f32[256,152]{1,0:T(8,128)S(1)} %all_gather.6.rm_ref) | copy-start | bytes 466948
  23.7 8.6 %copy-start.4 = (s32[64,27]{0,1:T(8,128)S(1)}, s32[64,27]{0,1:T(8,128)}, u32[]{:S(2)}) copy-start(s32[64,27]{0,1:T(8,128)} %param.17) | copy-start | bytes 20740
  23.7 9.3 %copy-start.5 = (s32[64,27]{0,1:T(8,128)S(1)}, s32[64,27]{0,1:T(8,128)}, u32[]{:S(2)}) copy-start(s32[64,27]{0,1:T(8,128)} %param.18) | copy-start | bytes 20740
  28.6 16.6 %copy-start.2 = (f32[8,16,560]{2,1,0:T(8,128)}, f32[8,16,560]{2,1,0:T(8,128)S(1)}, u32[]{:S(2)}) copy-start(f32[8,16,560]{2,1,0:T(8,128)S(1)} %all-to-all-done.1) | copy-start | bytes 860164
  28.6 18.3 %all-to-all-start = ((f32[8,64,152]{2,1,0:T(8,128)}), f32[8,64,152]{2,1,0:T(8,128)S(1)}, u32[]{:S(2)}, u32[]{:S(2)}) async-start(f32[8,64,152]{2,1,0:T(8,128)} %bitcast), calls=%async_computation | async-start | bytes 1048576 | tf_op jit(solution)/shard_map/all_to_all | solution.py:119
  46.9 0.8 %copy-start.1 = (f32[8,64,152]{2,1,0:T(8,128)}, f32[8,64,152]{2,1,0:T(8,128)S(1)}, u32[]{:S(2)}) copy-start(f32[8,64,152]{2,1,0:T(8,128)S(1)} %all-to-all-done) | copy-start | bytes 933892

commit v2 on v1

v2 whole, which is shorter than its diff:
```python
import functools

import jax
import jax.numpy as jnp
from jax import lax
from jax.experimental import pallas as pl
from jax.experimental.pallas import tpu as pltpu
from jax.sharding import PartitionSpec as P

NCAP = 16
LANES = 128
SUB = 8
F32 = jnp.float32
BF16 = jnp.bfloat16
VMEM = pl.BlockSpec(memory_space=pltpu.VMEM)
SMEM = pl.BlockSpec(memory_space=pltpu.SMEM)
HBM = pl.BlockSpec(memory_space=pltpu.HBM)


def cdiv(a, b):
    return -(-a // b)


def log2(n):
    assert n & (n - 1) == 0, n
    return n.bit_length() - 1


def split(x):
    hi = x.astype(BF16)
    return hi, (x - hi.astype(F32)).astype(BF16)


def mm(a, b):
    return lax.dot_general(a, b, (((1,), (0,)), ((), ())), preferred_element_type=F32)


def dot3(x, w):
    wh, wl = split(w)
    xh, xl = split(x)
    both = mm(jnp.concatenate([xh, xl], axis=0), wh)
    n = x.shape[0]
    return both[:n] + both[n:] + mm(xh, wl)


class Plan:
    def __init__(self, multi, cheb, ghost_rows, far_src, near_src, far_ops, near_ops, groups):
        self.targets, self.p = multi.shape
        self.q = cheb.shape[1]
        self.members, self.cap = ghost_rows.shape
        self.ncap = NCAP
        self.far, self.near = far_src.shape[1], near_src.shape[1]
        self.fcls, self.ncls = far_ops.shape[0], near_ops.shape[0]
        self.range = self.targets * groups
        self.halves = 2 if groups % 2 == 0 else 1
        self.fc, self.nc = self.cap // self.halves, self.ncap // self.halves
        self.ftable = self.range + self.members * self.cap
        self.ntable = self.targets + self.members * self.ncap
        self.fhi, self.nhi = cdiv(self.ftable, LANES), cdiv(self.ntable, LANES)
        self.nrows = cdiv(self.nhi * self.ncls, SUB) * SUB
        self.rows = cdiv(self.fhi * self.fcls + self.nrows, 16) * 16
        self.near_at = cdiv(self.far, 64) * 64
        self.slots = cdiv(self.near_at + self.near, LANES) * LANES
        self.pf, self.pt = divmod(self.p, LANES)
        self.width = self.p + self.q
        self.qf = cdiv(self.width, LANES) - self.pf
        self.step = 1 << (self.pt - 1).bit_length()
        self.per = LANES // self.step
        self.tail_rows = self.fc // self.per
        self.at_tail = self.pf * self.fc
        self.at_cheb = self.at_tail + self.tail_rows
        self.block = self.at_cheb + self.qf * self.nc
        assert self.tail_rows % SUB == 0 and self.nc % SUB == 0


def pack_kernel(d, par_ref, ghost_ref, table_ref, send_ref, tail_ref):
    par = par_ref[0]
    lane = lax.broadcasted_iota(jnp.int32, (d.tail_rows, LANES), 1)
    first = d.pf * LANES

    def body(r, carry):
        for c in range(d.fc):
            row = table_ref[pl.ds(ghost_ref[r, par * d.fc + c], 1), :]
            for j in range(d.pf):
                send_ref[r, j * d.fc + c:j * d.fc + c + 1, :] = row[:, j * LANES:(j + 1) * LANES]
            tail_ref[c:c + 1, :] = row[:, first:first + LANES]
        merged = jnp.zeros((d.tail_rows, LANES), F32)
        for g in range(d.per):
            part = pltpu.roll(tail_ref[g * d.tail_rows:(g + 1) * d.tail_rows, :], (g * d.step) % LANES, 1)
            merged = jnp.where((lane >= g * d.step) & (lane < g * d.step + d.pt), part, merged)
        send_ref[r, d.at_tail:d.at_cheb, :] = merged
        for c in range(d.nc):
            row = table_ref[pl.ds(ghost_ref[r, par * d.nc + c], 1), :]
            for j in range(d.qf):
                at = (d.pf + j) * LANES
                n = min(LANES, d.width - at)
                send_ref[r, d.at_cheb + j * d.nc + c:d.at_cheb + j * d.nc + c + 1, :n] = row[:, at:at + n]
        return carry

    lax.fori_loop(0, d.members, body, 0)


def counts_kernel(d, par_ref, cnt_ref, fsrc_ref, fkind_ref, nsrc_ref, nkind_ref, wf_ref, wn_ref, c_ref, lo_ref):
    group = 4
    par = par_ref[0]

    def place(src, own, cap, part):
        n = src - own
        c = n & (cap - 1)
        half = (c >> log2(part)) ^ par if d.halves == 2 else 0
        ghost = own + half * (d.members * part) + (n >> log2(cap)) * part + (c & (part - 1))
        return jnp.where(n < 0, src, ghost)

    fsrc = place(fsrc_ref[...], d.range, d.cap, d.fc)
    nsrc = place(nsrc_ref[...], d.targets, d.ncap, d.nc)
    c_ref[...] = jnp.full(c_ref.shape, -1, jnp.int32)
    lo_ref[...] = jnp.zeros(lo_ref.shape, jnp.int32)
    c_ref[:, :d.far] = (fsrc >> 7) * d.fcls + fkind_ref[...]
    lo_ref[:, :d.far] = fsrc & (LANES - 1)
    c_ref[:, d.near_at:d.near_at + d.near] = d.fhi * d.fcls + (nsrc >> 7) * d.ncls + nkind_ref[...]
    lo_ref[:, d.near_at:d.near_at + d.near] = nsrc & (LANES - 1)
    lane = lax.broadcasted_iota(jnp.int32, (1, d.slots), 1)
    row_id = lax.broadcasted_iota(jnp.int32, (d.rows, d.slots), 0)
    lo_id = lax.broadcasted_iota(jnp.int32, (LANES, d.slots), 0)

    def body(step, carry):
        for i in range(group):
            t = step * group + i
            live = (lane < cnt_ref[t]) | (lane >= d.near_at)
            c_row = jnp.where(live, c_ref[pl.ds(t, 1), :], -1)
            one_c = jnp.where(row_id == c_row, 1.0, 0.0).astype(BF16)
            one_lo = jnp.where(lo_id == lo_ref[pl.ds(t, 1), :], 1.0, 0.0).astype(BF16)
            w = lax.dot_general(one_c, one_lo, (((1,), (1,)), ((), ())), preferred_element_type=F32)
            at = pl.multiple_of(t * d.fcls, d.fcls)
            for h in range(d.fhi):
                wf_ref[pl.ds(at, d.fcls), h * LANES:(h + 1) * LANES] = w[h * d.fcls:(h + 1) * d.fcls].astype(BF16)
            wn_ref[pl.ds(pl.multiple_of(t * d.nrows, d.nrows), d.nrows), :] = (
                w[d.fhi * d.fcls:d.fhi * d.fcls + d.nrows])
        return carry

    lax.fori_loop(0, d.targets // group, body, 0)


def field_kernel(d, *refs):
    hbm, out_ref, vm, fs_ref, sem = refs[:9], refs[9], refs[10:19], refs[19], refs[20]
    copies = [pltpu.make_async_copy(hbm[i], vm[i], sem.at[i]) for i in range(9)]
    for copy in copies:
        copy.start()
    wf_ref, own_ref, pair_ref, multi_ref, wn_ref, cheb_ref, fops_ref, l2t_ref, nops_ref = vm
    got = (own_ref, pair_ref)[:d.halves]
    for i in range(4):
        copies[i].wait()
    far_sum = jnp.zeros((d.targets * d.fcls, d.p), F32)
    at = 0
    for part in (multi_ref,) + got:
        if part is multi_ref:
            rows = part[:, :d.p]
        else:
            cut = [part[:, j * d.fc:(j + 1) * d.fc, :].reshape(-1, LANES) for j in range(d.pf)]
            tail = part[:, d.at_tail:d.at_cheb, :].reshape(-1, LANES)
            tails = [pltpu.roll(tail, (-g * d.step) % LANES, 1).reshape(d.members, d.tail_rows, LANES)
                     for g in range(d.per)]
            tails = jnp.concatenate(tails, axis=1).reshape(-1, LANES)[:, :d.pt]
            rows = jnp.concatenate(cut + [tails], axis=1)
        rh, rl = split(rows)
        w = wf_ref[:, at:at + rows.shape[0]]
        far_sum += mm(w, rh) + mm(w, rl)
        at += rows.shape[0]
    cuts = [(at, min(at + LANES, d.p)) for at in range(0, d.p, LANES)]
    for i, (first, last) in enumerate(cuts):
        fs_ref[i, :, :last - first] = far_sum[:, first:last]
    copies[6].wait()
    local = jnp.zeros((d.targets, d.p), F32)
    for k in range(d.fcls):
        x = [fs_ref[i, pl.ds(k, d.targets, stride=d.fcls), :][:, :last - first] for i, (first, last) in enumerate(cuts)]
        local += dot3(jnp.concatenate(x, axis=1), fops_ref[k])
    for i in (4, 5):
        copies[i].wait()
    tables = [cheb_ref[...]]
    for part in got:
        cut = [part[:, d.at_cheb + j * d.nc:d.at_cheb + (j + 1) * d.nc, :].reshape(-1, LANES) for j in range(d.qf)]
        tables.append(jnp.concatenate(cut, axis=1)[:, d.pt:d.pt + d.q])
    th, tl = split(jnp.concatenate(tables, axis=0))
    sums = jnp.zeros((d.ncls * d.targets, d.q), F32)
    for h in range(d.nhi):
        first, last = h * LANES, min((h + 1) * LANES, d.ntable)
        w = jnp.concatenate(
            [wn_ref[pl.ds(h * d.ncls + k, d.targets, stride=d.nrows), :] for k in range(d.ncls)], axis=0
        ).astype(BF16)[:, :last - first]
        sums += mm(w, th[first:last]) + mm(w, tl[first:last])
    copies[7].wait()
    acc = dot3(local, l2t_ref[...])
    copies[8].wait()
    for k in range(d.ncls):
        acc += dot3(sums[k * d.targets:(k + 1) * d.targets], nops_ref[k])
    out_ref[...] = acc


def shards(groups, multipoles, chebyshev, ghost_rows, far_src, far_kind, far_count, near_src, near_kind,
           far_ops, near_ops, local_to_target):
    d = Plan(multipoles, chebyshev, ghost_rows, far_src, near_src, far_ops, near_ops, groups)
    packed = jnp.concatenate([multipoles, chebyshev], axis=1)
    table = lax.all_gather(packed, "grp", axis=0, tiled=True)
    parity = (lax.axis_index("grp") & 1).astype(jnp.int32).reshape(1)
    send = pl.pallas_call(
        functools.partial(pack_kernel, d),
        out_shape=jax.ShapeDtypeStruct((d.members, d.block, LANES), F32),
        in_specs=[SMEM, SMEM, VMEM],
        out_specs=VMEM,
        scratch_shapes=[pltpu.VMEM((d.fc, LANES), F32)],
        compiler_params=pltpu.CompilerParams(vmem_limit_bytes=16 << 20),
        name="pack",
    )(parity, ghost_rows, table)
    got = lax.all_to_all(send, "morton", split_axis=0, concat_axis=0, tiled=True)
    wf, wn = pl.pallas_call(
        functools.partial(counts_kernel, d),
        out_shape=(
            jax.ShapeDtypeStruct((d.targets * d.fcls, d.fhi * LANES), BF16),
            jax.ShapeDtypeStruct((d.targets * d.nrows, LANES), F32),
        ),
        in_specs=[SMEM, SMEM] + [VMEM] * 4,
        out_specs=(VMEM,) * 2,
        scratch_shapes=[pltpu.VMEM((d.targets, d.slots), jnp.int32)] * 2,
        cost_estimate=pl.CostEstimate(flops=20_000_000_000, transcendentals=0, bytes_accessed=2 << 20),
        name="counts",
    )(parity, far_count, far_src, far_kind, near_src, near_kind)
    got, wf, wn = lax.optimization_barrier((got, wf, wn))
    if d.halves == 2:
        pair = lax.ppermute(got, "grp", [(i, i ^ 1) for i in range(groups)])
    else:
        pair = got
    inputs = (wf, got, pair, table, wn, chebyshev, far_ops, local_to_target, near_ops)
    return pl.pallas_call(
        functools.partial(field_kernel, d),
        out_shape=jax.ShapeDtypeStruct((d.targets, d.q), F32),
        in_specs=[HBM] * 9,
        out_specs=VMEM,
        scratch_shapes=[pltpu.VMEM(x.shape, x.dtype) for x in inputs]
        + [pltpu.VMEM((cdiv(d.p, LANES), d.targets * d.fcls, LANES), F32), pltpu.SemaphoreType.DMA((9,))],
        name="field",
    )(*inputs)


def solution(mesh):
    both = P(("morton", "grp"), None)
    in_specs = (both, both, P("morton", None), both, both, P(("morton", "grp")), both, both, P(), P(), P())
    return jax.shard_map(functools.partial(shards, mesh.shape["grp"]), mesh=mesh, in_specs=in_specs,
                         out_specs=both, check_vma=False)
```

time: 57.8 us -> 41.8 us (0.72)
  blocking collectives: 15.4 us -> 10.1 us
  Pallas kernels: 21.3 us -> 16.6 us
  starting transfers between devices: 9.44 us -> 5.81 us
  local copies, waits for them, and re-layouts: 6.12 us -> 2.84 us
  waiting for transfers between devices: 4.42 us -> 5.02 us
    all_gather x2 -> x1, blocking collectives: 15.4 us -> 10.1 us  [shards(): table = lax.all_gather(packed, 'grp', axis=0, tiled=True)]
    pallas_call x2 -> x3, Pallas kernels: 21.3 us -> 16.6 us  [the longest x1 8.06 us: shards(): pl.pallas_call(functools.partial(field_kernel, d), out_shape=jax.ShapeDty...]
    gather x2 -> x0, local copies, waits for them, and re-layouts: 3.77 us -> none  [the longest x1 2.24 us: shards(): range_multi[ghost_rows]]
    all_to_all x2 -> x1, starting transfers between devices: 9.44 us -> 5.81 us  [shards(): lax.all_to_all(send, 'morton', split_axis=0, concat_axis=0, tiled=True)]
    ppermute x0 -> x1, waiting for transfers between devices: none -> 1.63 us  [shards(): pair = lax.ppermute(got, 'grp', [(i, i ^ 1) for i in range(groups)])]
    concatenate x0 -> x1, other arithmetic: none -> 1.04 us  [shards(): packed = jnp.concatenate([multipoles, chebyshev], axis=1)]
    all_to_all x2 -> x1, waiting for transfers between devices: 4.42 us -> 3.4 us  [shards(): lax.all_to_all(send, 'morton', split_axis=0, concat_axis=0, tiled=True)]
    select_n x2 -> x0, other arithmetic: 0.76 us -> none  [the longest x1 0.76 us: shards(): range_cheb[near_rows]]
  transfers between devices with their start and end apart: 2 -> 2, of which waited for: 2 -> 2; matrix products, arithmetic and copies ran while one was open for 6% -> 3% of each run, Pallas kernels for 20% -> 14%
where the time goes in v2:
time: 41.8 us; the launch traced here: 41.4 us
  Pallas kernels  16.6 us (40%)
  blocking collectives  10.1 us (24%)
  starting transfers between devices  5.81 us (14%)
  waiting for transfers between devices  5.02 us (12%)
  local copies, waits for them, and re-layouts  2.84 us (7%)
  other arithmetic  1.04 us (2%)
    all_gather x1, blocking collectives, shards(): table = lax.all_gather(packed, 'grp', axis=0, tiled=True)  10.1 us
    pallas_call x1, Pallas kernels, shards(): pl.pallas_call(functools.partial(field_kernel, d), out_shape=jax.ShapeDty...  8.06 us
    pallas_call x1, Pallas kernels, shards(): pl.pallas_call(functools.partial(counts_kernel, d), out_shape=(jax.ShapeD...  5.99 us
    all_to_all x1, starting transfers between devices, shards(): lax.all_to_all(send, 'morton', split_axis=0, concat_axis=0, tiled=True)  5.81 us
    all_to_all x1, waiting for transfers between devices, shards(): lax.all_to_all(send, 'morton', split_axis=0, concat_axis=0, tiled=True)  3.4 us
    unnamed x14, local copies, waits for them, and re-layouts  2.84 us
    pallas_call x1, Pallas kernels, shards(): pl.pallas_call(functools.partial(pack_kernel, d), out_shape=jax.ShapeDtyp...  2.56 us
    ppermute x1, waiting for transfers between devices, shards(): pair = lax.ppermute(got, 'grp', [(i, i ^ 1) for i in range(groups)])  1.63 us
  transfers between devices with their start and end apart: 2, of which 2 were waited for; matrix products, arithmetic and copies ran while one was open for 3% of the time, Pallas kernels for 14%

profile of v2, /device:TPU:0, one launch (start us, length us, event | category | flops | bytes accessed | tf_op | source)
XLA Modules:
  0.0 41.4 jit_solution(3239450641504109131)
XLA Ops:
  0.0 0.0 copy-start.4
  0.0 0.0 copy-start.5
  0.0 1.0 %pad_maximum_fusion = f32[64,712]{1,0:T(8,128)S(1)} fusion(f32[64,560]{1,0:T(8,128)} %refs_5_.1, f32[64,152]{1,0:T(8,128)} %param.11), kind=kLoop, calls=%fused_computation | loop fusion | flops 45568 | bytes 364544 | tf_op jit(solution)/shard_map/concatenate | solution.py:202
  1.0 10.1 %all_gather.3.table_ref.refs_3_ = f32[256,712]{1,0:T(8,128)S(1)} all-gather(f32[64,712]{1,0:T(8,128)S(1)} %pad_maximum_fusion), channel_id=1, replica_groups=mesh['morton'=8,'grp'=4] {'grp'}, dimensions={0}, use_global_device_ids=true | all-gather | bytes 911360 | tf_op jit(solution)/shard_map/all_gather | solution.py:203
  11.2 0.0 copy-start
  11.2 0.0 copy-start.1
  11.2 0.7 %copy-done.1 = s32[8,64]{1,0:T(8,128)S(1)} copy-done((s32[8,64]{1,0:T(8,128)S(1)}, s32[8,64]{1,0:T(8,128)}, u32[]{:S(2)}) %copy-start.1) | copy-done | bytes 2072
  11.8 2.6 %pack.1 = f32[8,80,128]{2,1,0:T(8,128)} custom-call(s32[1]{0:T(128)} %bitcast.par_ref, s32[8,64]{1,0:T(8,128)S(1)} %copy-done.1, f32[256,712]{1,0:T(8,128)S(1)} %all_gather.3.table_ref.refs_3_), custom_call_target="tpu_custom_call" | custom-call | tf_op jit(solution)/shard_map/pack/pallas_call | solution.py:205
  14.4 5.8 %all-to-all-start = ((f32[8,80,128]{2,1,0:T(8,128)}), f32[8,80,128]{2,1,0:T(8,128)S(1)}, u32[]{:S(2)}, u32[]{:S(2)}) async-start(f32[8,80,128]{2,1,0:T(8,128)} %pack.1), calls=%async_computation | async-start | bytes 655360 | tf_op jit(solution)/shard_map/all_to_all | solution.py:214
  20.2 0.0 copy-done.4
  20.2 0.7 %copy.12.nsrc_ref = s32[64,27]{1,0:T(8,128)} copy(s32[64,27]{0,1:T(8,128)S(1)} %copy-done.4) | data formatting | bytes 13824 | tf_op args[6]
  20.9 0.0 copy-done.5
  20.9 0.7 %copy.13.nkind_ref = s32[64,27]{1,0:T(8,128)} copy(s32[64,27]{0,1:T(8,128)S(1)} %copy-done.5) | data formatting | bytes 13824 | tf_op args[7]
  21.6 6.0 %counts.1 = (bf16[1024,768]{1,0:T(8,128)(2,1)}, f32[512,128]{1,0:T(8,128)}) custom-call(s32[1]{0:T(128)} %bitcast.par_ref, s32[64]{0:T(128)} %cnt_ref.1, s32[64,189]{1,0:T(8,128)} %fsrc_ref.1, s32[64,189]{1,0:T(8,128)} %fkind_ref.1, s32[64,27]{1,0:T(8,128)} %copy.12.nsrc_ref, s32[64,27]{1,0:T(8,128)} %copy.13.nkind_ref), custom_call_target="tpu_custom_call" | custom-call | flops 20000000000 | bytes 2097152 | tf_op jit(solution)/shard_map/counts/pallas_call | solution.py:215
  27.6 0.0 copy-done
  27.6 3.4 %all-to-all-done.refs_1_ = f32[8,80,128]{2,1,0:T(8,128)S(1)} async-done(((f32[8,80,128]{2,1,0:T(8,128)}), f32[8,80,128]{2,1,0:T(8,128)S(1)}, u32[]{:S(2)}, u32[]{:S(2)}) %all-to-all-start) | async-done | bytes 327712 | tf_op jit(solution)/shard_map/all_to_all | solution.py:214
  31.0 0.0 copy-start.2
  31.0 0.0 collective-permute-start
  31.0 1.6 %collective-permute-done.refs_2_ = f32[8,80,128]{2,1,0:T(8,128)S(1)} collective-permute-done((f32[8,80,128]{2,1,0:T(8,128)S(1)}, f32[8,80,128]{2,1,0:T(8,128)S(1)}, u32[]{:S(2)}, u32[]{:S(2)}) %collective-permute-start) | collective-permute-done | bytes 327712 | tf_op jit(solution)/shard_map/ppermute | solution.py:229
  32.6 0.0 copy-done.2
  32.6 0.0 copy-start.3
  32.6 0.7 %copy-done.3 = f32[8,80,128]{2,1,0:T(8,128)} copy-done((f32[8,80,128]{2,1,0:T(8,128)}, f32[8,80,128]{2,1,0:T(8,128)S(1)}, u32[]{:S(2)}) %copy-start.3) | copy-done | bytes 327704
  33.4 8.1 %field.1 = f32[64,560]{1,0:T(8,128)} custom-call(bf16[1024,768]{1,0:T(8,128)(2,1)} %get-tuple-element.12.refs_0_, f32[8,80,128]{2,1,0:T(8,128)} %copy-done.2, f32[8,80,128]{2,1,0:T(8,128)} %copy-done.3, f32[256,712]{1,0:T(8,128)} %copy-done, f32[512,128]{1,0:T(8,128)} %get-tuple-element.14.refs_4_, f32[64,560]{1,0:T(8,128)} %refs_5_.1, ...), custom_call_target="tpu_custom_call" | custom-call | tf_op jit(solution)/shard_map/field/pallas_call | solution.py:233
Async XLA Ops:
  0.0 20.2 %copy-start.4 = (s32[64,27]{0,1:T(8,128)S(1)}, s32[64,27]{0,1:T(8,128)}, u32[]{:S(2)}) copy-start(s32[64,27]{0,1:T(8,128)} %param.17) | copy-start | bytes 20740
  0.0 20.9 %copy-start.5 = (s32[64,27]{0,1:T(8,128)S(1)}, s32[64,27]{0,1:T(8,128)}, u32[]{:S(2)}) copy-start(s32[64,27]{0,1:T(8,128)} %param.18) | copy-start | bytes 20740
  11.2 16.4 %copy-start = (f32[256,712]{1,0:T(8,128)}, f32[256,712]{1,0:T(8,128)S(1)}, u32[]{:S(2)}) copy-start(f32[256,712]{1,0:T(8,128)S(1)} %all_gather.3.table_ref.refs_3_) | copy-start | bytes 2187268
  11.2 0.7 %copy-start.1 = (s32[8,64]{1,0:T(8,128)S(1)}, s32[8,64]{1,0:T(8,128)}, u32[]{:S(2)}) copy-start(s32[8,64]{1,0:T(8,128)} %ghost_ref.1) | copy-start | bytes 6148
  14.4 16.6 %all-to-all-start = ((f32[8,80,128]{2,1,0:T(8,128)}), f32[8,80,128]{2,1,0:T(8,128)S(1)}, u32[]{:S(2)}, u32[]{:S(2)}) async-start(f32[8,80,128]{2,1,0:T(8,128)} %pack.1), calls=%async_computation | async-start | bytes 655360 | tf_op jit(solution)/shard_map/all_to_all | solution.py:214
  31.0 1.6 %copy-start.2 = (f32[8,80,128]{2,1,0:T(8,128)}, f32[8,80,128]{2,1,0:T(8,128)S(1)}, u32[]{:S(2)}) copy-start(f32[8,80,128]{2,1,0:T(8,128)S(1)} %all-to-all-done.refs_1_) | copy-start | bytes 983044
  31.0 1.6 %collective-permute-start = (f32[8,80,128]{2,1,0:T(8,128)S(1)}, f32[8,80,128]{2,1,0:T(8,128)S(1)}, u32[]{:S(2)}, u32[]{:S(2)}) collective-permute-start(f32[8,80,128]{2,1,0:T(8,128)S(1)} %all-to-all-done.refs_1_), channel_id=1, source_target_pairs={{0,1},{1,0},{2,3},{3,2},{4,5},{5,4},{6,7},{7,6},{8,9},{9,8},{10,11... | collective-permute-start | bytes 983048 | tf_op jit(solution)/shard_map/ppermute | solution.py:229
  32.6 0.7 %copy-start.3 = (f32[8,80,128]{2,1,0:T(8,128)}, f32[8,80,128]{2,1,0:T(8,128)S(1)}, u32[]{:S(2)}) copy-start(f32[8,80,128]{2,1,0:T(8,128)S(1)} %collective-permute-done.refs_2_) | copy-start | bytes 983044
